TPU v7x, 8 devices: a whole 2x2x1 slice. The times are simulated.
8 devices in a mesh: batch: 1 (over z), row: 2 (over y), col: 4 (over x, core).
Axes of the slice: x: 2, y: 2, z: 1, core: 2. Of those that a mesh axis runs over, the one named last changes fastest.
Arguments:
- l_mat: bfloat16 [8192, 8192], P(('batch', 'row'), 'col')
- b_mat: bfloat16 [8192, 16384], P(('batch', 'row'), 'col')
Outputs:
- output: bfloat16 [8192, 16384], P(('batch', 'row'), 'col')
All inputs are finite; a program needn't handle non-finite values.
Results may differ from a plain program's by a relative error of at most 0.001.
Values are sent between devices in bfloat16 or wider.
A program may use at most 1 GiB of HBM per device.

v0:
```python
import jax
import jax.numpy as jnp
from jax import lax
from jax.sharding import PartitionSpec as P


def solution(mesh):
    block_spec = P(('batch', 'row'), 'col')

    def local_product(l_block, b_block):
        l_strip = lax.all_gather(l_block, 'col', axis=1, tiled=True)
        b_strip = lax.all_gather(b_block, 'row', axis=0, tiled=True)
        result = jnp.dot(l_strip, b_strip, preferred_element_type=jnp.float32)
        return result.astype(b_block.dtype)

    return jax.shard_map(local_product, mesh=mesh, in_specs=(block_spec, block_spec), out_specs=block_spec, check_vma=False)
```

profile of v0, /device:TPU:0, one launch (start us, length us, event | category | flops | bytes accessed | tf_op | source)
XLA Modules:
  0.0 1464.3 jit_solution(11735091502837677984)
XLA Ops:
  6.5 0.0 all-gather.5.cloned.1.call-start
  6.5 0.7 all-gather.5.cloned.1.call-update
  7.3 0.0 all-gather.3.cloned.1.call-start
  7.3 0.7 all-gather.3.cloned.1.call-update
  8.0 766.9 %all-gather.5.cloned.1.call-done = bf16[8192,4096]{1,0:T(8,128)(2,1)} async-done(((bf16[4096,4096]{1,0:T(8,128)(2,1)}), bf16[8192,4096]{1,0:T(8,128)(2,1)}) %all-gather.5.cloned.1.call-update) | async-done | bytes 67108880 | tf_op jit(solution)/shard_map/all_gather | solution.py:12
  774.9 391.2 %all-gather.3.cloned.1.call-done = bf16[4096,8192]{1,0:T(8,128)(2,1)} async-done(((bf16[4096,2048]{1,0:T(8,128)(2,1)}), bf16[4096,8192]{1,0:T(8,128)(2,1)}) %all-gather.3.cloned.1.call-update) | async-done | bytes 67108880 | tf_op jit(solution)/shard_map/all_gather | solution.py:11
  1166.1 291.4 %convolution_convert_fusion = bf16[4096,4096]{1,0:T(8,128)(2,1)} fusion(bf16[4096,8192]{1,0:T(8,128)(2,1)} %all-gather.3.cloned.1.call-done, bf16[8192,4096]{1,0:T(8,128)(2,1)} %all-gather.5.cloned.1.call-done), kind=kOutput, calls=%fused_computation | convolution fusion | flops 274894684160 | bytes 167772160 | tf_op jit(solution)/shard_map/dot_general | solution.py:13
Async XLA Ops:
  6.5 768.3 %all-gather.5.cloned.1.call-start = ((), (), s32[]{:S(2)}) async-start(), calls=%async_computation.1 | async-start | bytes 100663296 | tf_op jit(solution)/shard_map/all_gather | solution.py:12
  7.3 1158.8 %all-gather.3.cloned.1.call-start = ((), (), s32[]{:S(2)}) async-start(), calls=%async_computation | async-start | bytes 83886080 | tf_op jit(solution)/shard_map/all_gather | solution.py:11
Sparse Core Ops, SparseCore 0:
  8.8 765.9 all-gather.4
  776.4 389.6 all-gather.2
where the time goes:
time: 1460 us
  waiting for transfers between devices  1160 us (79%)
  matrix products  291 us (20%)
    all_gather x1, waiting for transfers between devices, local_product(): b_strip = lax.all_gather(b_block, 'row', axis=0, tiled=True)  767 us
    all_gather x1, waiting for transfers between devices, local_product(): l_strip = lax.all_gather(l_block, 'col', axis=1, tiled=True)  391 us
    dot_general x1, matrix products, local_product(): result = jnp.dot(l_strip, b_strip, preferred_element_type=jnp.float32)  291 us
  transfers between devices with their start and end apart: 2, of which 2 were waited for; matrix products, arithmetic and copies ran while one was open for 0% of the time, Pallas kernels for 0%

commit v1 on v0

v1 whole, which is shorter than its diff:
```python
import functools

import jax
import jax.numpy as jnp
import numpy as np
from jax import lax
from jax.experimental import pallas as pl
from jax.experimental.pallas import tpu as pltpu
from jax.sharding import PartitionSpec as P


TM = 512
KB = 1024
NBUF = 8
WIDTHS = (512, 1024, 1024, 512, 512, 256, 256)


def plan(half):
    tables = []
    for row in range(2):
        steps, seen = [], set()
        for r in range(half // TM):
            n_k = row * (half // KB) + -(-(r + 1) * TM // KB)
            for k in range(n_k):
                steps.append((r, k, int(k == 0), int(k == n_k - 1), int(k not in seen)))
                seen.add(k)
        tables.append(steps)
    return tables


def chunk_kernel(half, depth, col0, width, counts, tab, info, l0, l1, l2, l3, b_loc, b_rec, *rest):
    x_out, bv, lv, acc, ov, lsem, bsem, osem = rest[-8:]
    row, col = info[0], info[1]
    stride = max(counts) * 5
    n = jnp.where(row == 0, counts[0], counts[1])
    per = depth // KB
    nb = half // KB

    def field(t, f):
        return tab[row * stride + t * 5 + f]

    def l_start(t, slot):
        r, k = field(t, 0), field(t, 1)
        which = lax.bitwise_xor(k // per, col)
        for i, ref in enumerate((l0, l1, l2, l3)):
            @pl.when(which == i)
            def _():
                pltpu.make_async_copy(
                    ref.at[pl.ds(r * TM, TM), pl.ds(lax.rem(k, per) * KB, KB)],
                    lv.at[slot], lsem.at[slot]).start()

    def b_copy(ref, src, dst):
        return pltpu.make_async_copy(
            ref.at[pl.ds(src * KB, KB), pl.ds(col0 if ref is b_loc else 0, width)],
            bv.at[pl.ds(dst * KB, KB), :], bsem.at[dst])

    def o_copy(r, slot):
        return pltpu.make_async_copy(
            ov.at[slot], x_out.at[pl.ds(r * TM, TM), pl.ds(col0, width)], osem.at[slot])

    for k in range(nb):
        @pl.when(row == 0)
        def _():
            b_copy(b_loc, k, k).start()

        @pl.when(row == 1)
        def _():
            b_copy(b_rec, k, k).start()

        l_start(k, k)
    for k in range(nb):
        @pl.when(row == 1)
        def _():
            b_copy(b_loc, k, nb + k).start()
    for t in range(nb, NBUF - 1):
        l_start(t, t)

    def step(t, _):
        slot = lax.rem(t, NBUF)
        r, k = field(t, 0), field(t, 1)

        @pl.when(t + NBUF - 1 < n)
        def _():
            l_start(t + NBUF - 1, lax.rem(t + NBUF - 1, NBUF))

        @pl.when(field(t, 4) == 1)
        def _():
            pltpu.make_async_copy(b_loc.at[pl.ds(0, KB), pl.ds(col0, width)],
                                  bv.at[pl.ds(0, KB), :], bsem.at[k]).wait()

        pltpu.make_async_copy(l0.at[pl.ds(0, TM), pl.ds(0, KB)], lv.at[slot], lsem.at[slot]).wait()

        part = functools.partial(jnp.dot, preferred_element_type=jnp.float32)
        first = field(t, 2)
        rows_k = pl.ds(pl.multiple_of(k * KB, KB), KB)

        @pl.when(first == 1)
        def _():
            acc[...] = part(lv[slot], bv[rows_k, :])

        @pl.when(first == 0)
        def _():
            acc[...] += part(lv[slot], bv[rows_k, :])

        @pl.when(field(t, 3) == 1)
        def _():
            oslot = lax.rem(r, 2)

            @pl.when(r >= 2)
            def _():
                o_copy(r - 2, oslot).wait()

            ov[oslot] = acc[...].astype(ov.dtype)
            o_copy(r, oslot).start()

        return 0

    lax.fori_loop(0, n, step, 0)
    last = half // TM
    o_copy(last - 2, (last - 2) % 2).wait()
    o_copy(last - 1, (last - 1) % 2).wait()


def solution(mesh):
    block_spec = P(('batch', 'row'), 'col')
    x_swap = [(0, 2), (1, 3), (2, 0), (3, 1)]
    core_swap = [(0, 1), (1, 0), (2, 3), (3, 2)]

    def product(l_block, b_block):
        half, depth = l_block.shape
        tables = plan(half)
        counts = tuple(len(s) for s in tables)
        flat = np.zeros((2, max(counts), 5), np.int32)
        for row in range(2):
            flat[row, :counts[row]] = tables[row]
        tab = jnp.asarray(flat.reshape(-1))
        info = jnp.stack([lax.axis_index('row'), lax.axis_index('col')]).astype(jnp.int32)

        lc = lax.ppermute(l_block, 'col', core_swap)
        lx = lax.ppermute(l_block, 'col', x_swap)
        recv, col0, source = [], 0, b_block
        for width in WIDTHS:
            piece = source[:, col0:col0 + width]
            piece, source = lax.optimization_barrier((piece, source))
            recv.append(lax.ppermute(piece, 'row', [(0, 1)]))
            col0 += width
        lxc = lax.ppermute(lx, 'col', core_swap)

        x, col0 = None, 0
        for j, width in enumerate(WIDTHS):
            hbm = pl.BlockSpec(memory_space=pltpu.HBM)
            operands = [tab, info, l_block, lc, lx, lxc, b_block, recv[j]]
            if x is not None:
                operands.append(x)
            x = pl.pallas_call(
                functools.partial(chunk_kernel, half, depth, col0, width, counts),
                out_shape=jax.ShapeDtypeStruct(b_block.shape, b_block.dtype),
                grid_spec=pltpu.PrefetchScalarGridSpec(
                    num_scalar_prefetch=2, grid=(1,),
                    in_specs=[hbm] * (len(operands) - 2), out_specs=hbm,
                    scratch_shapes=[
                        pltpu.VMEM((2 * half, width), b_block.dtype),
                        pltpu.VMEM((NBUF, TM, KB), l_block.dtype),
                        pltpu.VMEM((TM, width), jnp.float32),
                        pltpu.VMEM((2, TM, width), b_block.dtype),
                        pltpu.SemaphoreType.DMA((NBUF,)),
                        pltpu.SemaphoreType.DMA((2 * half // KB,)),
                        pltpu.SemaphoreType.DMA((2,)),
                    ]),
                input_output_aliases={} if j == 0 else {8: 0},
                cost_estimate=pl.CostEstimate(flops=max(counts) * 2 * TM * KB * width,
                                              bytes_accessed=max(counts) * 2 * TM * KB, transcendentals=0),
            )(*operands)
            col0 += width
        return x

    return jax.shard_map(product, mesh=mesh, in_specs=(block_spec, block_spec), out_specs=block_spec, check_vma=False)
```

time: 1460 us -> 1130 us (0.77); the launches traced: 1460 us -> 1110 us
  matrix products: 291 us -> 0 us
  waiting for transfers between devices: 1160 us -> 876 us
  Pallas kernels: 0 us -> 150 us
  starting transfers between devices: 0.04 us -> 51.9 us
  local copies, waits for them, and re-layouts: 0 us -> 34.8 us
    all_gather x2 -> x0, waiting for transfers between devices: 1160 us -> none  [the longest x1 767 us: local_product(): b_strip = lax.all_gather(b_block, 'row', axis=0, tiled=True)]
    ppermute x0 -> x10, waiting for transfers between devices: none -> 876 us  [the longest x7 516 us: product(): recv.append(lax.ppermute(piece, 'row', [(0, 1)]))]
    dot_general x1 -> x0, matrix products: 291 us -> none  [local_product(): result = jnp.dot(l_strip, b_strip, preferred_element_type=jnp.float32)]
    pallas_call x0 -> x7, Pallas kernels: none -> 150 us  [product(): pl.pallas_call(functools.partial(chunk_kernel, half, depth, col0, width,...]
    ppermute x0 -> x10, starting transfers between devices: none -> 51.9 us  [the longest x7 48.6 us: product(): recv.append(lax.ppermute(piece, 'row', [(0, 1)]))]
    slice x0 -> x7, local copies, waits for them, and re-layouts: none -> 34.8 us  [product(): piece = source[:, col0:col0 + width]]
  transfers between devices with their start and end apart: 2 -> 10, of which waited for: 2 -> 7; matrix products, arithmetic and copies ran while one was open for 0% -> 3% of each run, Pallas kernels for 0% -> 12%
where the time goes in v1:
time: 1130 us; the launch traced here: 1110 us
  waiting for transfers between devices  876 us (78%)
  Pallas kernels  150 us (13%)
  starting transfers between devices  51.9 us (5%)
  local copies, waits for them, and re-layouts  34.8 us (3%)
    ppermute x7, waiting for transfers between devices, product(): recv.append(lax.ppermute(piece, 'row', [(0, 1)]))  516 us
    ppermute x1, waiting for transfers between devices, product(): lx = lax.ppermute(l_block, 'col', x_swap)  361 us
    pallas_call x7, Pallas kernels, product(): pl.pallas_call(functools.partial(chunk_kernel, half, depth, col0, width,...  150 us
    ppermute x7, starting transfers between devices, product(): recv.append(lax.ppermute(piece, 'row', [(0, 1)]))  48.6 us
    slice x7, local copies, waits for them, and re-layouts, product(): piece = source[:, col0:col0 + width]  34.8 us
  transfers between devices with their start and end apart: 10, of which 7 were waited for; matrix products, arithmetic and copies ran while one was open for 3% of the time, Pallas kernels for 12%

profile of v1, /device:TPU:0, one launch (start us, length us, event | category | flops | bytes accessed | tf_op | source)
XLA Modules:
  0.0 1113.7 jit_solution(11606003942315328308)
XLA Ops:
  0.0 3.3 collective-permute-start.1
  3.3 360.5 %collective-permute-done.1.l2 = bf16[4096,2048]{1,0:T(8,128)(2,1)} collective-permute-done((bf16[4096,2048]{1,0:T(8,128)(2,1)}, bf16[4096,2048]{1,0:T(8,128)(2,1)}, u32[]{:S(2)}, u32[]{:S(2)}) %collective-permute-start.1) | collective-permute-done | bytes 16777248 | tf_op jit(solution)/shard_map/ppermute | solution.py:140
  363.8 4.5 slice.21
  368.3 7.7 slice.22
  376.0 6.9 collective-permute-start.8
  382.9 3.3 collective-permute-start.9
  386.1 7.6 slice.23
  393.7 4.5 collective-permute-start.7
  398.2 4.4 slice.24
  402.7 4.4 slice.25
  407.1 3.1 slice.26
  410.2 3.1 slice.27
  413.3 0.7 pad_add_fusion.info
  413.9 236.8 %collective-permute-done.9.b_rec = bf16[4096,512]{1,0:T(8,128)(2,1)} collective-permute-done((bf16[4096,512]{1,0:T(8,128)(2,1)}, bf16[4096,512]{1,0:T(8,128)(2,1)}, u32[]{:S(2)}, u32[]{:S(2)}) %collective-permute-start.9) | collective-permute-done | bytes 4194336 | tf_op jit(solution)/shard_map/ppermute | solution.py:145
  650.7 6.4 collective-permute-start.6
  657.0 3.3 collective-permute-start.5
  660.3 0.0 collective-permute-done.2.l3
  660.3 2.6 collective-permute-start.4
  663.0 19.7 %shard_map.37.rest_0_ = bf16[4096,4096]{1,0:T(8,128)(2,1)} custom-call(s32[520]{0:T(1024)} %constant.11.clone.tab, s32[2]{0:T(128)} %pad_add_fusion.info, bf16[4096,2048]{1,0:T(8,128)(2,1)} %l0.13, bf16[4096,2048]{1,0:T(8,128)(2,1)} %collective-permute-done.l1, bf16[4096,2048]{1,0:T(8,128)(2,1)} %collective-permute-done.1.l2, ...), custom_call_target="tpu_custom_call" | custom-call | flops 27917287424 | bytes 54525952 | tf_op jit(solution)/shard_map/pallas_call | solution.py:155
  682.6 0.0 collective-permute-done.8.b_rec
  682.7 21.7 %collective-permute-start.3 = (bf16[4096,256]{1,0:T(8,128)(2,1)}, bf16[4096,256]{1,0:T(8,128)(2,1)}, u32[]{:S(2)}, u32[]{:S(2)}) collective-permute-start(bf16[4096,256]{1,0:T(8,128)(2,1)} %slice.27), channel_id=1, source_target_pairs={{0,4},{1,5},{2,6},{3,7}} | collective-permute-start | bytes 6291464 | tf_op jit(solution)/shard_map/ppermute | solution.py:145
  704.3 31.6 %shard_map.38.rest_0_ = bf16[4096,4096]{1,0:T(8,128)(2,1)} custom-call(s32[520]{0:T(1024)} %constant.11.clone.tab, s32[2]{0:T(128)} %pad_add_fusion.info, bf16[4096,2048]{1,0:T(8,128)(2,1)} %l0.13, bf16[4096,2048]{1,0:T(8,128)(2,1)} %collective-permute-done.l1, bf16[4096,2048]{1,0:T(8,128)(2,1)} %collective-permute-done.1.l2, ...), custom_call_target="tpu_custom_call", output_to_operand_aliasing={{}: (8, {})} | custom-call | flops 55834574848 | bytes 54525952 | tf_op jit(solution)/shard_map/pallas_call | solution.py:155
  735.9 94.6 %collective-permute-done.7.b_rec = bf16[4096,1024]{1,0:T(8,128)(2,1)} collective-permute-done((bf16[4096,1024]{1,0:T(8,128)(2,1)}, bf16[4096,1024]{1,0:T(8,128)(2,1)}, u32[]{:S(2)}, u32[]{:S(2)}) %collective-permute-start.7) | collective-permute-done | bytes 8388640 | tf_op jit(solution)/shard_map/ppermute | solution.py:145
  830.4 31.6 %shard_map.39.rest_0_ = bf16[4096,4096]{1,0:T(8,128)(2,1)} custom-call(s32[520]{0:T(1024)} %constant.11.clone.tab, s32[2]{0:T(128)} %pad_add_fusion.info, bf16[4096,2048]{1,0:T(8,128)(2,1)} %l0.13, bf16[4096,2048]{1,0:T(8,128)(2,1)} %collective-permute-done.l1, bf16[4096,2048]{1,0:T(8,128)(2,1)} %collective-permute-done.1.l2, ...), custom_call_target="tpu_custom_call", output_to_operand_aliasing={{}: (8, {})} | custom-call | flops 55834574848 | bytes 54525952 | tf_op jit(solution)/shard_map/pallas_call | solution.py:155
  862.0 58.3 %collective-permute-done.6.b_rec = bf16[4096,512]{1,0:T(8,128)(2,1)} collective-permute-done((bf16[4096,512]{1,0:T(8,128)(2,1)}, bf16[4096,512]{1,0:T(8,128)(2,1)}, u32[]{:S(2)}, u32[]{:S(2)}) %collective-permute-start.6) | collective-permute-done | bytes 4194336 | tf_op jit(solution)/shard_map/ppermute | solution.py:145
  920.3 19.7 %shard_map.40.rest_0_ = bf16[4096,4096]{1,0:T(8,128)(2,1)} custom-call(s32[520]{0:T(1024)} %constant.11.clone.tab, s32[2]{0:T(128)} %pad_add_fusion.info, bf16[4096,2048]{1,0:T(8,128)(2,1)} %l0.13, bf16[4096,2048]{1,0:T(8,128)(2,1)} %collective-permute-done.l1, bf16[4096,2048]{1,0:T(8,128)(2,1)} %collective-permute-done.1.l2, ...), custom_call_target="tpu_custom_call", output_to_operand_aliasing={{}: (8, {})} | custom-call | flops 27917287424 | bytes 54525952 | tf_op jit(solution)/shard_map/pallas_call | solution.py:155
  940.0 70.2 %collective-permute-done.5.b_rec = bf16[4096,512]{1,0:T(8,128)(2,1)} collective-permute-done((bf16[4096,512]{1,0:T(8,128)(2,1)}, bf16[4096,512]{1,0:T(8,128)(2,1)}, u32[]{:S(2)}, u32[]{:S(2)}) %collective-permute-start.5) | collective-permute-done | bytes 4194336 | tf_op jit(solution)/shard_map/ppermute | solution.py:145
  1010.2 19.7 %shard_map.41.rest_0_ = bf16[4096,4096]{1,0:T(8,128)(2,1)} custom-call(s32[520]{0:T(1024)} %constant.11.clone.tab, s32[2]{0:T(128)} %pad_add_fusion.info, bf16[4096,2048]{1,0:T(8,128)(2,1)} %l0.13, bf16[4096,2048]{1,0:T(8,128)(2,1)} %collective-permute-done.l1, bf16[4096,2048]{1,0:T(8,128)(2,1)} %collective-permute-done.1.l2, ...), custom_call_target="tpu_custom_call", output_to_operand_aliasing={{}: (8, {})} | custom-call | flops 27917287424 | bytes 54525952 | tf_op jit(solution)/shard_map/pallas_call | solution.py:155
  1029.9 25.2 %collective-permute-done.4.b_rec = bf16[4096,256]{1,0:T(8,128)(2,1)} collective-permute-done((bf16[4096,256]{1,0:T(8,128)(2,1)}, bf16[4096,256]{1,0:T(8,128)(2,1)}, u32[]{:S(2)}, u32[]{:S(2)}) %collective-permute-start.4) | collective-permute-done | bytes 2097184 | tf_op jit(solution)/shard_map/ppermute | solution.py:145
  1055.2 13.9 %shard_map.42.rest_0_ = bf16[4096,4096]{1,0:T(8,128)(2,1)} custom-call(s32[520]{0:T(1024)} %constant.11.clone.tab, s32[2]{0:T(128)} %pad_add_fusion.info, bf16[4096,2048]{1,0:T(8,128)(2,1)} %l0.13, bf16[4096,2048]{1,0:T(8,128)(2,1)} %collective-permute-done.l1, bf16[4096,2048]{1,0:T(8,128)(2,1)} %collective-permute-done.1.l2, ...), custom_call_target="tpu_custom_call", output_to_operand_aliasing={{}: (8, {})} | custom-call | flops 13958643712 | bytes 54525952 | tf_op jit(solution)/shard_map/pallas_call | solution.py:155
  1069.0 30.6 %collective-permute-done.3.b_rec = bf16[4096,256]{1,0:T(8,128)(2,1)} collective-permute-done((bf16[4096,256]{1,0:T(8,128)(2,1)}, bf16[4096,256]{1,0:T(8,128)(2,1)}, u32[]{:S(2)}, u32[]{:S(2)}) %collective-permute-start.3) | collective-permute-done | bytes 2097184 | tf_op jit(solution)/shard_map/ppermute | solution.py:145
  1099.6 13.9 %shard_map.43 = bf16[4096,4096]{1,0:T(8,128)(2,1)} custom-call(s32[520]{0:T(1024)} %constant.11.clone.tab, s32[2]{0:T(128)} %pad_add_fusion.info, bf16[4096,2048]{1,0:T(8,128)(2,1)} %l0.13, bf16[4096,2048]{1,0:T(8,128)(2,1)} %collective-permute-done.l1, bf16[4096,2048]{1,0:T(8,128)(2,1)} %collective-permute-done.1.l2, ...), custom_call_target="tpu_custom_call", output_to_operand_aliasing={{}: (8, {})} | custom-call | flops 13958643712 | bytes 54525952 | tf_op jit(solution)/shard_map/pallas_call | solution.py:155
  (3 shorter events, 0.0 us)
Async XLA Ops:
  0.0 363.8 %collective-permute-start.1 = (bf16[4096,2048]{1,0:T(8,128)(2,1)}, bf16[4096,2048]{1,0:T(8,128)(2,1)}, u32[]{:S(2)}, u32[]{:S(2)}) collective-permute-start(bf16[4096,2048]{1,0:T(8,128)(2,1)} %l0.13), channel_id=1, source_target_pairs={{0,2},{1,3},{2,0},{3,1},{4,6},{5,7},{6,4},{7,5}} | collective-permute-start | bytes 50331656 | tf_op jit(solution)/shard_map/ppermute | solution.py:140
  3.3 653.7 %collective-permute-start = (bf16[4096,2048]{1,0:T(8,128)(2,1)}, bf16[4096,2048]{1,0:T(8,128)(2,1)}, u32[]{:S(2)}, u32[]{:S(2)}) collective-permute-start(bf16[4096,2048]{1,0:T(8,128)(2,1)} %l0.13), channel_id=1, source_target_pairs={{0,1},{1,0},{2,3},{3,2},{4,5},{5,4},{6,7},{7,6}} | collective-permute-start | bytes 50331656 | tf_op jit(solution)/shard_map/ppermute | solution.py:139
  363.8 296.5 %collective-permute-start.2 = (bf16[4096,2048]{1,0:T(8,128)(2,1)}, bf16[4096,2048]{1,0:T(8,128)(2,1)}, u32[]{:S(2)}, u32[]{:S(2)}) collective-permute-start(bf16[4096,2048]{1,0:T(8,128)(2,1)} %collective-permute-done.1.l2), channel_id=1, source_target_pairs={{0,1},{1,0},{2,3},{3,2},{4,5},{5,4},{6,7},{7,6}} | collective-permute-start | bytes 50331656 | tf_op jit(solution)/shard_map/ppermute | solution.py:147
  376.0 306.7 %collective-permute-start.8 = (bf16[4096,1024]{1,0:T(8,128)(2,1)}, bf16[4096,1024]{1,0:T(8,128)(2,1)}, u32[]{:S(2)}, u32[]{:S(2)}) collective-permute-start(bf16[4096,1024]{1,0:T(8,128)(2,1)} %slice.22), channel_id=1, source_target_pairs={{0,4},{1,5},{2,6},{3,7}} | collective-permute-start | bytes 25165832 | tf_op jit(solution)/shard_map/ppermute | solution.py:145
  382.9 267.8 %collective-permute-start.9 = (bf16[4096,512]{1,0:T(8,128)(2,1)}, bf16[4096,512]{1,0:T(8,128)(2,1)}, u32[]{:S(2)}, u32[]{:S(2)}) collective-permute-start(bf16[4096,512]{1,0:T(8,128)(2,1)} %slice.21), channel_id=1, source_target_pairs={{0,4},{1,5},{2,6},{3,7}} | collective-permute-start | bytes 12582920 | tf_op jit(solution)/shard_map/ppermute | solution.py:145
  393.7 436.7 %collective-permute-start.7 = (bf16[4096,1024]{1,0:T(8,128)(2,1)}, bf16[4096,1024]{1,0:T(8,128)(2,1)}, u32[]{:S(2)}, u32[]{:S(2)}) collective-permute-start(bf16[4096,1024]{1,0:T(8,128)(2,1)} %slice.23), channel_id=1, source_target_pairs={{0,4},{1,5},{2,6},{3,7}} | collective-permute-start | bytes 25165832 | tf_op jit(solution)/shard_map/ppermute | solution.py:145
  650.7 269.6 %collective-permute-start.6 = (bf16[4096,512]{1,0:T(8,128)(2,1)}, bf16[4096,512]{1,0:T(8,128)(2,1)}, u32[]{:S(2)}, u32[]{:S(2)}) collective-permute-start(bf16[4096,512]{1,0:T(8,128)(2,1)} %slice.24), channel_id=1, source_target_pairs={{0,4},{1,5},{2,6},{3,7}} | collective-permute-start | bytes 12582920 | tf_op jit(solution)/shard_map/ppermute | solution.py:145
  657.0 353.2 %collective-permute-start.5 = (bf16[4096,512]{1,0:T(8,128)(2,1)}, bf16[4096,512]{1,0:T(8,128)(2,1)}, u32[]{:S(2)}, u32[]{:S(2)}) collective-permute-start(bf16[4096,512]{1,0:T(8,128)(2,1)} %slice.25), channel_id=1, source_target_pairs={{0,4},{1,5},{2,6},{3,7}} | collective-permute-start | bytes 12582920 | tf_op jit(solution)/shard_map/ppermute | solution.py:145
  660.3 394.8 %collective-permute-start.4 = (bf16[4096,256]{1,0:T(8,128)(2,1)}, bf16[4096,256]{1,0:T(8,128)(2,1)}, u32[]{:S(2)}, u32[]{:S(2)}) collective-permute-start(bf16[4096,256]{1,0:T(8,128)(2,1)} %slice.26), channel_id=1, source_target_pairs={{0,4},{1,5},{2,6},{3,7}} | collective-permute-start | bytes 6291464 | tf_op jit(solution)/shard_map/ppermute | solution.py:145
  682.7 417.0 %collective-permute-start.3 = (bf16[4096,256]{1,0:T(8,128)(2,1)}, bf16[4096,256]{1,0:T(8,128)(2,1)}, u32[]{:S(2)}, u32[]{:S(2)}) collective-permute-start(bf16[4096,256]{1,0:T(8,128)(2,1)} %slice.27), channel_id=1, source_target_pairs={{0,4},{1,5},{2,6},{3,7}} | collective-permute-start | bytes 6291464 | tf_op jit(solution)/shard_map/ppermute | solution.py:145
